TPU v7x, 32 devices: a whole 2x2x4 slice. The times are simulated.
32 devices in a mesh: grp: 2 (over y), seq: 4 (over z), dp: 2 (over x), tp: 2 (over core).
Axes of the slice: x: 2, y: 2, z: 4, core: 2. Of those that a mesh axis runs over, the one named last changes fastest.
Arguments:
- query_image: bfloat16 [4, 1024, 2048], P(('grp', 'dp'), ('seq', 'tp')), parts along dimension 0, may hold values from -8 to 8
- key_image: bfloat16 [4, 1024, 2048], P(('grp', 'dp'), ('seq', 'tp')), parts along dimension 0, may hold values from -8 to 8
- value_image: bfloat16 [4, 1024, 2048], P(('grp', 'dp'), ('seq', 'tp')), parts along dimension 0, may hold values from -6 to 6
- query_text: bfloat16 [4, 128, 2048], P(('grp', 'dp'), ('seq', 'tp')), parts along dimension 0, may hold values from -6 to 6
- key_text: bfloat16 [4, 128, 2048], P(('grp', 'dp'), ('seq', 'tp')), parts along dimension 0, may hold values from -6 to 6
- value_text: bfloat16 [4, 128, 2048], P(('grp', 'dp'), ('seq', 'tp')), parts along dimension 0, may hold values from -6 to 6
- image_query_gain: float32 [128], replicated, may hold values from 1 to 6
- image_key_gain: float32 [128], replicated, may hold values from 1 to 6
- text_query_gain: float32 [128], replicated, may hold values from 1.2 to 2.5
- text_key_gain: float32 [128], replicated, may hold values from 1.2 to 2.5
- text_length: int32 [4], P(('grp', 'dp')), parts along dimension 0, may hold values from 1 to 128
- strata: int32 [4], P(('grp', 'dp')), parts along dimension 0, may hold values from 0 to 63
- image_state: bfloat16 [4, 1024, 3072], P(('grp', 'dp'), ('seq', 'tp')), parts along dimension 0, may hold values from -6 to 6
- target: bfloat16 [4, 1024, 3072], P(('grp', 'dp'), ('seq', 'tp')), parts along dimension 0, may hold values from -6 to 6
- out_weight: bfloat16 [2048, 3072], P('seq', 'tp'), may hold values from -0.125 to 0.125
- gate_table: bfloat16 [64, 3072], replicated, may hold values from -4 to 4
Outputs:
- velocity: bfloat16 [4, 1024, 3072], P(('grp', 'dp'), ('seq', 'tp')), parts along dimension 0
- text_attention: bfloat16 [4, 128, 2048], P(('grp', 'dp'), ('seq', 'tp')), parts along dimension 0
- flow_loss: float32 [2], P('grp'), parts along dimension 0
There are 2 independent parts, one for each index of `grp`. A program takes and returns all parts, laid end to end along the dimension named above; an argument that names none is the same for every part. Nothing has to cross between parts.
Inputs may be any that keep to these rules, and one draw needn't show every extreme that they name: `text_length`: text positions at or beyond a sample's length are padding and are not attended to.
All inputs are finite; a program needn't handle non-finite values.
Results may differ from a plain program's by a relative error of at most 0.012.
The roundings to bfloat16 on the way count: a program that leaves them out, or rounds other values in their place, can miss the bound.
Values may be sent and summed in bfloat16 or wider, within the bound.
No kernel may reach another device: no remote copies, remote signals or barrier semaphores. Data moves between devices by JAX's collectives and lax.ppermute only.
A program may use at most 64 MiB of HBM per device.

v0:
```python
import jax
import jax.numpy as jnp
from jax import lax
from jax.sharding import PartitionSpec as P


def head_norm(values, gain_vector):
    head_dim = gain_vector.shape[0]
    columns = values.shape[-1]
    shaped = values.astype(jnp.float32).reshape(values.shape[:-1] + (columns // head_dim, head_dim))
    inverse = lax.rsqrt(jnp.mean(shaped * shaped, axis=-1, keepdims=True) + 1e-06)
    return (shaped * inverse * gain_vector).reshape(values.shape).astype(jnp.bfloat16)


def attend(query_block, key_split, value_split, usable, factor):
    scores = (
        jnp.einsum("qhd,khd->hqk", query_block, key_split, preferred_element_type=jnp.float32)
        * factor
    )
    scores = jnp.where(usable[None, None, :], scores, -1e30)
    row_max = jnp.max(scores, axis=2, keepdims=True)
    powers = jnp.exp(scores - row_max)
    weights = (powers / jnp.sum(powers, axis=2, keepdims=True)).astype(jnp.bfloat16)
    return jnp.einsum(
        "hqk,khd->qhd", weights, value_split, preferred_element_type=jnp.float32
    ).astype(jnp.bfloat16)


def local(
    query_image,
    key_image,
    value_image,
    query_text,
    key_text,
    value_text,
    image_query_gain,
    image_key_gain,
    text_query_gain,
    text_key_gain,
    text_length,
    strata,
    image_state,
    target,
    out_weight,
    gate_table,
):
    samples = query_image.shape[0]
    image_count = query_image.shape[1]
    text_count = query_text.shape[1]
    local_rows = image_count + text_count
    head_dim = image_query_gain.shape[0]
    seq_count = lax.axis_size("seq")
    core_count = lax.axis_size("tp")
    queries = jnp.concatenate(
        [head_norm(query_text, text_query_gain), head_norm(query_image, image_query_gain)], axis=1
    )
    keys_local = jnp.concatenate(
        [head_norm(key_text, text_key_gain), head_norm(key_image, image_key_gain)], axis=1
    )
    values_local = jnp.concatenate([value_text, value_image], axis=1)
    key_index = jnp.arange(seq_count * core_count * local_rows, dtype=jnp.int32)
    within = key_index % local_rows
    query_heads, key_rows, value_rows = (
        lax.all_to_all(queries, "seq", split_axis=2, concat_axis=1, tiled=True),
        lax.all_to_all(keys_local, "seq", split_axis=2, concat_axis=1, tiled=True),
        lax.all_to_all(values_local, "seq", split_axis=2, concat_axis=1, tiled=True),
    )
    key_heads, value_heads = (
        lax.all_gather(key_rows, "tp", axis=1, tiled=True),
        lax.all_gather(value_rows, "tp", axis=1, tiled=True),
    )
    core_shard = key_index // (seq_count * local_rows)
    seq_shard = key_index // local_rows % seq_count
    text_place = (seq_shard * core_count + core_shard) * text_count + within
    usable = (within[None, :] >= text_count) | (text_place[None, :] < text_length[:, None])
    query_total = query_heads.shape[1]
    heads_device = query_heads.shape[2] // head_dim
    block_rows = query_total // 4
    factor = head_dim ** (-0.5)

    def one_sample(operands):
        query_rows, key_sample, value_sample, usable_row = operands
        blocks = query_rows.reshape(4, block_rows, heads_device, head_dim)
        key_split = key_sample.reshape(key_sample.shape[0], heads_device, head_dim)
        value_split = value_sample.reshape(value_sample.shape[0], heads_device, head_dim)

        def one_block(block):
            return attend(block, key_split, value_split, usable_row, factor)

        outputs = lax.map(one_block, blocks)
        return outputs.reshape(query_total, heads_device * head_dim)

    head_output = lax.map(one_sample, (query_heads, key_heads, value_heads, usable))
    attention = lax.all_to_all(head_output, "seq", split_axis=1, concat_axis=2, tiled=True)
    text_attention = attention[:, :text_count]
    model_width = gate_table.shape[1]
    image_rows = attention[:, text_count:].reshape(samples * image_count, attention.shape[2])
    both_cores = lax.all_gather(image_rows, "tp", axis=0, tiled=True)
    half_columns = jnp.dot(
        both_cores,
        lax.all_gather(out_weight, "seq", axis=0, tiled=True),
        preferred_element_type=jnp.float32,
    )
    branch = lax.all_to_all(
        half_columns.astype(jnp.bfloat16), "tp", split_axis=0, concat_axis=1, tiled=True
    ).astype(half_columns.dtype)
    table_rows = gate_table.shape[0]
    selector = (strata[:, None] == jnp.arange(table_rows, dtype=jnp.int32)[None, :]).astype(
        jnp.bfloat16
    )
    gate_rows = jnp.dot(selector, gate_table, preferred_element_type=jnp.float32)
    combined = image_state.astype(jnp.float32) + gate_rows[:, None, :] * branch.reshape(
        samples, image_count, model_width
    )
    error_terms = combined - target.astype(jnp.float32)
    partial_sum = jnp.sum(error_terms * error_terms)
    total_sum = lax.psum(partial_sum, ("seq", "dp", "tp"))
    element_count = (
        samples * image_count * model_width * seq_count * core_count * lax.axis_size("dp")
    )
    flow_loss = (total_sum / element_count).reshape(1)
    return (combined.astype(jnp.bfloat16), text_attention, flow_loss)


def solution(mesh):
    placed = (
        P(("grp", "dp"), ("seq", "tp"), None),
        P(("grp", "dp"), ("seq", "tp"), None),
        P(("grp", "dp"), ("seq", "tp"), None),
        P(("grp", "dp"), ("seq", "tp"), None),
        P(("grp", "dp"), ("seq", "tp"), None),
        P(("grp", "dp"), ("seq", "tp"), None),
        P(),
        P(),
        P(),
        P(),
        P(("grp", "dp")),
        P(("grp", "dp")),
        P(("grp", "dp"), ("seq", "tp"), None),
        P(("grp", "dp"), ("seq", "tp"), None),
        P("seq", "tp"),
        P(),
    )
    return jax.shard_map(
        local,
        mesh=mesh,
        in_specs=placed,
        out_specs=(
            P(("grp", "dp"), ("seq", "tp"), None),
            P(("grp", "dp"), ("seq", "tp"), None),
            P("grp"),
        ),
        check_vma=False,
    )
```

profile of v0, /device:TPU:0, one launch (start us, length us, event | category | flops | bytes accessed | tf_op | source)
XLA Modules:
  0.0 360.4 jit_solution(4217201155704315449)
XLA Ops:
  7.2 1.2 fusion.30
  10.8 1.6 copy.125
  12.4 0.5 broadcast.226
  12.9 11.6 %reduce.9 = bf16[2048,144]{1,0:T(8,128)(2,1)S(1)} reduce(bf16[2048,1,144]{2,1,0:T(2,128)(2,1)S(1)} %bitcast.85, bf16[]{:T(256)} %broadcast.226), dimensions={1}, to_apply=%bitcast.64.reduce_sub_computation | reduce | bytes 1179650
  24.6 2.3 reshape.298
  26.9 6.3 %all-to-all-start.1 = ((bf16[4,2,36864]{2,1,0:T(2,128)(2,1)}), bf16[4,2,36864]{2,1,0:T(2,128)(2,1)}, u32[]{:S(2)}, u32[]{:S(2)}) async-start(bf16[4,2,36864]{2,1,0:T(2,128)(2,1)} %reshape.298), calls=%async_computation.1 | async-start | bytes 1179648 | tf_op jit(solution)/shard_map/all_to_all | solution.py:65
  34.4 1.6 copy.129
  36.1 11.6 %reduce.10 = bf16[2048,144]{1,0:T(8,128)(2,1)S(1)} reduce(bf16[2048,1,144]{2,1,0:T(2,128)(2,1)S(1)} %bitcast.86, bf16[]{:T(256)} %broadcast.226), dimensions={1}, to_apply=%bitcast.66.reduce_sub_computation | reduce | bytes 1179650
  47.7 2.3 reshape.300
  50.1 5.1 %all-to-all-start.2 = ((bf16[4,2,36864]{2,1,0:T(2,128)(2,1)}), bf16[4,2,36864]{2,1,0:T(2,128)(2,1)S(1)}, u32[]{:S(2)}, u32[]{:S(2)}) async-start(bf16[4,2,36864]{2,1,0:T(2,128)(2,1)} %reshape.300), calls=%async_computation.2 | async-start | bytes 1179648 | tf_op jit(solution)/shard_map/all_to_all | solution.py:66
  55.2 3.8 %reshape.299 = bf16[2048,1,144]{2,1,0:T(2,128)(2,1)S(1)} reshape(bf16[4,2,36864]{2,1,0:T(2,128)(2,1)} %all-to-all-done.1) | data formatting | bytes 1179648
  59.0 3.3 copy.126
  62.3 2.0 all_to_all.64
  64.3 0.9 copy.127
  66.6 2.0 fusion.29
  68.6 1.9 all-to-all-done.2
  70.5 3.1 reshape.301
  73.6 3.3 copy.130
  76.9 2.1 all_to_all.68
  78.9 0.9 copy.131
  80.0 1.6 copy.120
  81.6 11.6 %reduce.8 = bf16[2048,144]{1,0:T(8,128)(2,1)S(1)} reduce(bf16[2048,1,144]{2,1,0:T(2,128)(2,1)S(1)} %bitcast.89, bf16[]{:T(256)} %broadcast.226), dimensions={1}, to_apply=%bitcast.62.reduce_sub_computation | reduce | bytes 1179650
  93.2 2.3 reshape.296
  95.6 3.5 all-to-all-start
  99.1 15.4 %all-to-all-done = bf16[4,2,36864]{2,1,0:T(2,128)(2,1)S(1)} async-done(((bf16[4,2,36864]{2,1,0:T(2,128)(2,1)}), bf16[4,2,36864]{2,1,0:T(2,128)(2,1)S(1)}, u32[]{:S(2)}, u32[]{:S(2)}) %all-to-all-start) | async-done | bytes 589856 | tf_op jit(solution)/shard_map/all_to_all | solution.py:64
  114.5 3.1 reshape.297
  117.6 1.2 copy.121
  119.5 1.7 copy.128
  121.2 0.7 copy.134
  121.9 1.7 copy.132
  123.6 1.4 copy.135
  125.0 26.5 %while.18 = (s32[]{:T(128)}, bf16[4,144,4,128]{3,2,1,0:T(4,128)(2,1)}, bf16[4,144,4,128]{3,2,0,1:T(4,128)(2,1)S(1)}, bf16[1152,4,128]{2,0,1:T(8,128)(2,1)S(1)}, ...) while((s32[]{:T(128)}, bf16[4,144,4,128]{3,2,1,0:T(4,128)(2,1)}, ...), condition=%wide.region_7.8_spmd.clone, body=%wide.region_4.7_spmd.clone.sunk | while | flops 343836288 | bytes 8559957 | solution.py:90
  125.1 0.7 fusion.58
  125.8 2.5 fusion.59
  128.3 2.7 fusion.60
  130.9 0.7 copy_dynamic-update-slice_fusion.2
  131.7 0.7 fusion.58
  132.4 2.5 fusion.59
  134.9 2.7 fusion.60
  137.6 0.7 copy_dynamic-update-slice_fusion.2
  138.3 0.7 fusion.58
  139.0 2.5 fusion.59
  141.5 2.7 fusion.60
  144.2 0.7 copy_dynamic-update-slice_fusion.2
  145.0 0.7 fusion.58
  145.6 2.5 fusion.59
  148.1 2.7 fusion.60
  150.8 0.7 copy_dynamic-update-slice_fusion.2
  151.5 3.6 broadcast_in_dim.23
  155.1 4.2 %reduce.11 = bf16[576,512]{1,0:T(8,128)(2,1)S(1)} reduce(bf16[576,1,512]{2,1,0:T(2,128)(2,1)S(1)} %bitcast.91, bf16[]{:T(256)} %broadcast.226), dimensions={1}, to_apply=%bitcast.68.reduce_sub_computation | reduce | bytes 1179650
  159.3 0.4 reshape.302
  159.8 17.8 %all_to_all.82 = bf16[4,2,36864]{2,1,0:T(2,128)(2,1)S(1)} all-to-all(bf16[4,2,36864]{2,1,0:T(2,128)(2,1)S(1)} %reshape.302), channel_id=1, replica_groups=mesh['grp'=2,'seq'=4,'dp'=2,'tp'=2] {'seq'}, dimensions={0} | all-to-all | bytes 1179648 | tf_op jit(solution)/shard_map/all_to_all | solution.py:94
  177.6 0.6 reshape.303
  178.4 0.8 slice.8
  179.3 0.5 all-gather.10.cloned.1.call-update
  180.7 0.6 slice.9
  181.3 6.3 %all-gather.12.cloned.1.call-done = bf16[1,256,2048]{2,1,0:T(8,128)(2,1)} async-done(((bf16[1,128,2048]{2,1,0:T(8,128)(2,1)}), bf16[1,256,2048]{2,1,0:T(8,128)(2,1)}) %all-gather.12.cloned.1.call-update) | async-done | bytes 1048592 | tf_op jit(solution)/shard_map/all_gather | solution.py:98
  187.5 118.0 %all-gather.10.cloned.1.call-done = bf16[2048,1536]{1,0:T(8,128)(2,1)} async-done(((bf16[512,1536]{1,0:T(8,128)(2,1)}), bf16[2048,1536]{1,0:T(8,128)(2,1)}) %all-gather.10.cloned.1.call-update) | async-done | bytes 6291472 | tf_op jit(solution)/shard_map/all_gather | solution.py:101
  305.5 4.9 %convolution_convert_fusion = bf16[256,1536]{1,0:T(8,128)(2,1)S(1)} fusion(bf16[2048,1536]{1,0:T(8,128)(2,1)} %all-gather.10.cloned.1.call-done, bf16[1,256,2048]{2,1,0:T(8,128)(2,1)} %all-gather.12.cloned.1.call-done), kind=kOutput, calls=%fused_computation.42 | convolution fusion | flops 1611005952 | bytes 8126464 | tf_op jit(solution)/shard_map/dot_general | solution.py:99
  310.4 4.4 %all_to_all.83 = bf16[2,128,1536]{2,1,0:T(8,128)(2,1)S(1)} all-to-all(bf16[2,128,1536]{2,1,0:T(8,128)(2,1)S(1)} %bitcast.105), channel_id=1, replica_groups=mesh['grp'=2,'seq'=4,'dp'=2,'tp'=2] {'tp'}, dimensions={0} | all-to-all | bytes 1572864 | tf_op jit(solution)/shard_map/all_to_all | solution.py:104
  315.0 1.2 copy.139
  316.2 1.4 reshape.291
  317.5 3.2 multiply_reduce_fusion
  320.8 31.3 %psum.7 = f32[]{:T(128)} all-reduce(f32[]{:T(128)} %get-tuple-element.125), channel_id=1, replica_groups=mesh['grp'=2,'seq'=4,'dp'=2,'tp'=2] {'seq','dp','tp'}, use_global_device_ids=true, to_apply=%region_9.10 | all-reduce | flops 1 | bytes 8 | tf_op jit(solution)/shard_map/psum | solution.py:117
  (84 shorter events, 6.4 us)
Async XLA Ops:
  7.2 173.3 %copy-start = (bf16[64,3072]{1,0:T(8,128)(2,1)S(1)}, bf16[64,3072]{1,0:T(8,128)(2,1)}, u32[]{:S(2)}) copy-start(bf16[64,3072]{1,0:T(8,128)(2,1)} %param.33) | copy-start | bytes 1179652
  9.1 0.7 copy-start.9
  9.1 0.8 copy-start.5
  9.5 0.8 copy-start.10
  9.5 1.1 copy-start.1
  24.5 8.7 %copy-start.2 = (bf16[1,128,2048]{2,1,0:T(8,128)(2,1)S(1)}, bf16[1,128,2048]{2,1,0:T(8,128)(2,1)}, u32[]{:S(2)}) copy-start(bf16[1,128,2048]{2,1,0:T(8,128)(2,1)} %param.18) | copy-start | bytes 1572868
  26.9 23.2 %all-to-all-start.1 = ((bf16[4,2,36864]{2,1,0:T(2,128)(2,1)}), bf16[4,2,36864]{2,1,0:T(2,128)(2,1)}, u32[]{:S(2)}, u32[]{:S(2)}) async-start(bf16[4,2,36864]{2,1,0:T(2,128)(2,1)} %reshape.298), calls=%async_computation.1 | async-start | bytes 1179648 | tf_op jit(solution)/shard_map/all_to_all | solution.py:65
  33.3 1.0 copy-start.4
  33.3 1.0 copy-start.8
  47.7 2.3 copy-start.6
  50.1 20.4 %all-to-all-start.2 = ((bf16[4,2,36864]{2,1,0:T(2,128)(2,1)}), bf16[4,2,36864]{2,1,0:T(2,128)(2,1)S(1)}, u32[]{:S(2)}, u32[]{:S(2)}) async-start(bf16[4,2,36864]{2,1,0:T(2,128)(2,1)} %reshape.300), calls=%async_computation.2 | async-start | bytes 1179648 | tf_op jit(solution)/shard_map/all_to_all | solution.py:66
  55.2 64.3 %all-gather.6.cloned.1.call-start = ((), (), s32[]{:S(2)}) async-start(), calls=%async_computation.5 | async-start | bytes 1769472 | tf_op jit(solution)/shard_map/all_gather | solution.py:69
  65.2 56.7 %all-gather.8.cloned.1.call-start = ((), (), s32[]{:S(2)}) async-start(), calls=%async_computation.6 | async-start | bytes 1769472 | tf_op jit(solution)/shard_map/all_gather | solution.py:70
  65.9 0.7 copy-start.11
  65.9 0.7 copy-start.12
  76.9 3.0 copy-start.7
  76.9 3.0 copy-start.3
  95.6 18.9 %all-to-all-start = ((bf16[4,2,36864]{2,1,0:T(2,128)(2,1)}), bf16[4,2,36864]{2,1,0:T(2,128)(2,1)S(1)}, u32[]{:S(2)}, u32[]{:S(2)}) async-start(bf16[4,2,36864]{2,1,0:T(2,128)(2,1)} %reshape.296), calls=%async_computation | async-start | bytes 1179648 | tf_op jit(solution)/shard_map/all_to_all | solution.py:64
  99.1 88.5 %all-gather.12.cloned.1.call-start = ((), (), s32[]{:S(2)}) async-start(), calls=%async_computation.8 | async-start | bytes 1572864 | tf_op jit(solution)/shard_map/all_gather | solution.py:98
  179.3 126.3 %all-gather.10.cloned.1.call-start = ((), (), s32[]{:S(2)}) async-start(), calls=%async_computation.7 | async-start | bytes 7864320 | tf_op jit(solution)/shard_map/all_gather | solution.py:101
Sparse Core Ops, SparseCore 0:
  65.4 10.6 all-gather.5
  80.0 8.7 all-gather.7
  179.4 8.1 all-gather.11
  189.0 116.4 all-gather.9
where the time goes:
time: 361 us; the launch traced here: 360 us
  waiting for transfers between devices  142 us (39%)
  local copies, waits for them, and re-layouts  57.3 us (16%)
  blocking collectives  53.5 us (15%)
  other arithmetic  49.7 us (14%)
  matrix products  25.7 us (7%)
  between operations  16.7 us (5%)
  starting transfers between devices  15.2 us (4%)
    all_gather x1, waiting for transfers between devices, local(): lax.all_gather(out_weight, 'seq', axis=0, tiled=True)  118 us
    unnamed x8, other arithmetic  40.4 us
    psum x1, blocking collectives, local(): total_sum = lax.psum(partial_sum, ('seq', 'dp', 'tp'))  31.3 us
    unnamed x42, local copies, waits for them, and re-layouts  22.5 us
    all_to_all x1, blocking collectives, local(): lax.all_to_all(head_output, 'seq', split_axis=1, concat_axis=2, tiled=True)  17.8 us
    all_to_all x1, waiting for transfers between devices, local(): lax.all_to_all(queries, 'seq', split_axis=2, concat_axis=1, tiled=True)  15.4 us
    dot_general x4, matrix products, attend(): jnp.einsum('hqk,khd->qhd', weights, value_split, preferred_element_type=j...  10.7 us
    sub x4, matrix products, attend(): powers = jnp.exp(scores - row_max)  9.95 us
  transfers between devices with their start and end apart: 7, of which 4 were waited for; matrix products, arithmetic and copies ran while one was open for 16% of the time, Pallas kernels for 0%

commit v1 on v0

v1 whole, which is shorter than its diff:
```python
import functools
import math

import jax
import jax.numpy as jnp
from jax import lax
from jax.experimental import pallas as pl
from jax.experimental.pallas import tpu as pltpu
from jax.sharding import PartitionSpec as P

VMEM = pltpu.MemorySpace.VMEM
SMEM = pltpu.MemorySpace.SMEM


def vmem_specs(count):
    return [pl.BlockSpec(memory_space=VMEM) for _ in range(count)]


def norm_rows(values, gain_row, head_dim):
    wide = values.astype(jnp.float32)
    inverse = lax.rsqrt(jnp.sum(wide * wide, axis=-1, keepdims=True) * (1.0 / head_dim) + 1e-06)
    return (wide * inverse * gain_row).astype(jnp.bfloat16)


def pack_kv_body(key_image, key_text, value_image, value_text, image_gain, text_gain, *outs, head_dim):
    count = len(outs)
    width = key_image.shape[1] // count
    text = key_text.shape[0]
    own = lax.axis_index("seq")
    for j, out in enumerate(outs):
        start = pl.multiple_of(lax.rem(own + j, count) * width, width)
        for h in range(width // head_dim):
            here = pl.ds(pl.multiple_of(start + h * head_dim, head_dim), head_dim)
            there = slice(h * head_dim, (h + 1) * head_dim)
            out[0, :text, there] = norm_rows(key_text[:, here], text_gain[...], head_dim)
            out[0, text:, there] = norm_rows(key_image[:, here], image_gain[...], head_dim)
        out[1, :text, :] = value_text[:, pl.ds(start, width)]
        out[1, text:, :] = value_image[:, pl.ds(start, width)]


def pack_q_body(query_image, query_text, image_gain, text_gain, *outs, head_dim):
    count = len(outs)
    width = query_image.shape[1] // count
    text = query_text.shape[0]
    own = lax.axis_index("seq")
    for j, out in enumerate(outs):
        start = pl.multiple_of(lax.rem(own + j, count) * width, width)
        for h in range(width // head_dim):
            here = pl.ds(pl.multiple_of(start + h * head_dim, head_dim), head_dim)
            there = slice(h * head_dim, (h + 1) * head_dim)
            out[:text, there] = norm_rows(query_text[:, here], text_gain[...], head_dim)
            out[text:, there] = norm_rows(query_image[:, here], image_gain[...], head_dim)


def attend_body(length, *refs, queries, pieces, cores, text, head_dim, kinds):
    query_refs = refs[:queries]
    kv_refs = refs[queries:queries + pieces]
    weight_refs = refs[queries + pieces:queries + pieces + cores]
    out_refs = refs[queries + pieces + cores:queries * 3 + pieces + cores]
    keys, values, heads_out = refs[queries * 3 + pieces + cores:]
    rows, width = query_refs[0].shape
    image = rows - text
    text_total = text * pieces
    ring = lax.axis_size("seq")
    own = lax.axis_index("seq")
    own_core = lax.axis_index("tp")
    for i, ref in enumerate(kv_refs):
        for target, plane in ((keys, 0), (values, 1)):
            target[i * text:(i + 1) * text, :] = ref[plane, :text, :]
            target[text_total + i * image:text_total + (i + 1) * image, :] = ref[plane, text:, :]
    lane = lax.broadcasted_iota(jnp.int32, (1, text_total), 1)
    position = lane
    for i in range(pieces):
        shard = lax.rem(own + ring - i // cores, ring)
        core = lax.rem(own_core + i % cores, cores)
        place = (shard * cores + core - i) * text
        inside = (lane >= i * text) & (lane < (i + 1) * text)
        position = jnp.where(inside, lane + place, position)
    usable = position < length[0]
    scale = head_dim ** (-0.5) * math.log2(math.e)
    for b, query in enumerate(query_refs):
        for h in range(width // head_dim):
            cols = slice(h * head_dim, (h + 1) * head_dim)
            raw = lax.dot_general(
                query[:, cols], keys[:, cols], (((1,), (1,)), ((), ())), preferred_element_type=jnp.float32
            )
            text_part = jnp.where(usable, raw[:, :text_total], -1e30)
            image_part = raw[:, text_total:]
            top = jnp.maximum(
                jnp.max(text_part, axis=1, keepdims=True), jnp.max(image_part, axis=1, keepdims=True)
            )
            text_power = jnp.exp2((text_part - top) * scale)
            image_power = jnp.exp2((image_part - top) * scale)
            total = jnp.sum(text_power, axis=1, keepdims=True) + jnp.sum(image_power, axis=1, keepdims=True)
            inverse = 1.0 / total
            weights = jnp.concatenate(
                [(text_power * inverse).astype(jnp.bfloat16), (image_power * inverse).astype(jnp.bfloat16)], axis=1
            )
            heads_out[:, cols] = jnp.dot(
                weights, values[:, cols], preferred_element_type=jnp.float32
            ).astype(jnp.bfloat16)
        out_refs[2 * b + 1][...] = heads_out[:text, :]
        half = weight_refs[0].shape[1]
        for c, weight in enumerate(weight_refs):
            start = pl.multiple_of(lax.rem(own_core + c, cores) * half, half)
            out_refs[2 * b][:, pl.ds(start, half)] = jnp.dot(
                heads_out[text:, :], weight[...], preferred_element_type=jnp.float32
            ).astype(kinds[b])


def finish_body(strata, own_part, *refs, arrivals, count):
    arrival_refs = refs[:arrivals]
    state, target, table = refs[arrivals:arrivals + 3]
    text_refs = refs[arrivals + 3:arrivals + 3 + count]
    velocity, text_out, loss = refs[arrivals + 3 + count:]
    own = lax.axis_index("seq")
    row = lax.broadcasted_iota(jnp.int32, table.shape, 0)
    gate = jnp.sum(jnp.where(row == strata[0], table[...].astype(jnp.float32), 0.0), axis=0, keepdims=True)
    branch = own_part[...]
    for ref in arrival_refs:
        branch = branch + ref[...].astype(jnp.float32)
    combined = state[...].astype(jnp.float32) + gate * branch
    velocity[...] = combined.astype(jnp.bfloat16)
    error = combined - target[...].astype(jnp.float32)
    loss[...] = jnp.sum(error * error).reshape(1, 1)
    width = text_out.shape[1] // count
    for j, ref in enumerate(text_refs):
        start = pl.multiple_of(lax.rem(own + count - j, count) * width, width)
        text_out[:, pl.ds(start, width)] = ref[...]


def shift(ring, amount):
    return [(i, (i + amount) % ring) for i in range(ring)]


def both_ways(ring, cores, amount):
    pairs = []
    for i in range(ring):
        for c in range(cores):
            step = amount if c % 2 == 0 else -amount
            pairs.append((i * cores + c, (i + step) % ring * cores + c))
    return pairs


def exchange(blocks, ring, cores):
    arrived = [None] * ring
    arrived[0] = blocks[0]
    middle = ring // 2 if ring % 2 == 0 else None
    if middle:
        halfway = blocks[middle]
        if middle > 1:
            halfway = lax.ppermute(halfway, ("seq", "tp"), both_ways(ring, cores, middle - 1))
    for j in range(1, (ring + 1) // 2):
        arrived[j] = lax.ppermute(blocks[j], "seq", shift(ring, j))
        arrived[ring - j] = lax.ppermute(blocks[ring - j], "seq", shift(ring, -j))
    if middle:
        arrived[middle] = lax.ppermute(halfway, ("seq", "tp"), both_ways(ring, cores, 1))
    return arrived


def all_sum(value, axes):
    for axis in axes:
        size = lax.axis_size(axis)
        if size & (size - 1):
            value = lax.psum(value, axis)
            continue
        step = 1
        while step < size:
            value = value + lax.ppermute(value, axis, [(i, i ^ step) for i in range(size)])
            step *= 2
    return value


def one_sample(
    query_image, key_image, value_image, query_text, key_text, value_text,
    gains, text_length, strata, image_state, target, weights, gate_table,
):
    image, columns = query_image.shape
    text = query_text.shape[0]
    rows = image + text
    model_width = gate_table.shape[1]
    head_dim = gains[0].shape[1]
    ring = lax.axis_size("seq")
    cores = lax.axis_size("tp")
    width = columns // ring
    bf16 = jnp.bfloat16
    kv_blocks = pl.pallas_call(
        functools.partial(pack_kv_body, head_dim=head_dim),
        out_shape=[jax.ShapeDtypeStruct((2, rows, width), bf16)] * ring,
        in_specs=vmem_specs(6),
        out_specs=vmem_specs(ring),
        name="pack_kv",
    )(key_image, key_text, value_image, value_text, gains[1], gains[3])
    kv_arrived = exchange(kv_blocks, ring, cores)
    q_blocks = pl.pallas_call(
        functools.partial(pack_q_body, head_dim=head_dim),
        out_shape=[jax.ShapeDtypeStruct((rows, width), bf16)] * ring,
        in_specs=vmem_specs(4),
        out_specs=vmem_specs(ring),
        name="pack_q",
    )(query_image, query_text, gains[0], gains[2])
    q_arrived = exchange(q_blocks, ring, cores)
    pieces = []
    for piece in kv_arrived:
        pieces.append(piece)
        for c in range(1, cores):
            pieces.append(lax.ppermute(piece, "tp", [((i + c) % cores, i) for i in range(cores)]))

    def attend(blocks, kinds, name):
        shapes = []
        for kind in kinds:
            shapes.append(jax.ShapeDtypeStruct((image, model_width), kind))
            shapes.append(jax.ShapeDtypeStruct((text, width), bf16))
        keys_shape = (rows * ring * cores, width)
        out = pl.pallas_call(
            functools.partial(
                attend_body, queries=len(blocks), pieces=len(pieces), cores=cores,
                text=text, head_dim=head_dim, kinds=kinds,
            ),
            out_shape=shapes,
            in_specs=[pl.BlockSpec(memory_space=SMEM)] + vmem_specs(len(blocks) + len(pieces) + cores),
            out_specs=vmem_specs(len(shapes)),
            scratch_shapes=[
                pltpu.VMEM(keys_shape, bf16), pltpu.VMEM(keys_shape, bf16), pltpu.VMEM((rows, width), bf16)
            ],
            name=name,
        )(text_length, *blocks, *pieces, *weights)
        return out[0::2], out[1::2]

    return attend, q_arrived


def local(
    query_image, key_image, value_image, query_text, key_text, value_text,
    image_query_gain, image_key_gain, text_query_gain, text_key_gain,
    text_length, strata, image_state, target, out_weight, gate_table,
):
    samples, image, _ = query_image.shape
    text = query_text.shape[1]
    model_width = gate_table.shape[1]
    ring = lax.axis_size("seq")
    cores = lax.axis_size("tp")
    up_count = ring // 2
    down_count = (ring - 1) // 2
    up_core = lax.axis_index("tp") % 2 == 0
    gains = [g.reshape(1, -1) for g in (image_query_gain, image_key_gain, text_query_gain, text_key_gain)]
    weights = [out_weight]
    for c in range(1, cores):
        weights.append(lax.ppermute(out_weight, "tp", [((i + c) % cores, i) for i in range(cores)]))
    velocities, texts, losses = [], [], []
    for s in range(samples):
        attend, q = one_sample(
            query_image[s], key_image[s], value_image[s], query_text[s], key_text[s], value_text[s],
            gains, text_length[s:s + 1], strata[s:s + 1], image_state[s], target[s], weights, gate_table,
        )
        parts = {}
        text_rows = {}
        first = [ring // 2] if ring % 2 == 0 else []
        rest = [j for j in range(ring) if j not in first]
        if first:
            (parts_first,), (text_first,) = attend([q[first[0]]], [jnp.bfloat16], "attend_far")
            parts[first[0]] = parts_first
            text_rows[first[0]] = text_first
        rest_parts, rest_text = attend(
            [q[j] for j in rest], [jnp.float32 if j == 0 else jnp.bfloat16 for j in rest], "attend_rest"
        )
        for j, part, t in zip(rest, rest_parts, rest_text):
            parts[j] = part
            text_rows[j] = t

        def toward(sign, j):
            up = parts[(ring - j) % ring]
            down = parts[j % ring]
            if up is down:
                return up
            pick_up = up_core if sign == 1 else jnp.logical_not(up_core)
            return jnp.where(pick_up, up, down)

        arrivals = []
        for sign, count in ((1, up_count), (-1, down_count)):
            carried = None
            for j in range(count, 0, -1):
                part = toward(sign, j)
                if carried is not None:
                    part = (part.astype(jnp.float32) + carried.astype(jnp.float32)).astype(jnp.bfloat16)
                carried = lax.ppermute(part, ("seq", "tp"), both_ways(ring, cores, sign))
            if carried is not None:
                arrivals.append(carried)
        text_arrived = [text_rows[0]] + [
            lax.ppermute(text_rows[j], "seq", shift(ring, -j)) for j in range(1, ring)
        ]
        text_down = [text_arrived[(ring - j) % ring] for j in range(ring)]
        velocity, text_out, loss = pl.pallas_call(
            functools.partial(finish_body, arrivals=len(arrivals), count=ring),
            out_shape=[
                jax.ShapeDtypeStruct((image, model_width), jnp.bfloat16),
                jax.ShapeDtypeStruct((text, query_image.shape[2]), jnp.bfloat16),
                jax.ShapeDtypeStruct((1, 1), jnp.float32),
            ],
            in_specs=[pl.BlockSpec(memory_space=SMEM)] + vmem_specs(1 + len(arrivals) + 3 + ring),
            out_specs=vmem_specs(3),
            name="finish",
        )(strata[s:s + 1], parts[0], *arrivals, image_state[s], target[s], gate_table, *text_down)
        velocities.append(velocity)
        texts.append(text_out)
        losses.append(loss)
    total = sum(losses[1:], losses[0])
    total = all_sum(total, ("tp", "dp", "seq"))
    element_count = samples * image * model_width * ring * cores * lax.axis_size("dp")
    flow_loss = (total / element_count).reshape(1)
    return jnp.stack(velocities), jnp.stack(texts), flow_loss


def solution(mesh):
    tokens = P(("grp", "dp"), ("seq", "tp"), None)
    placed = (tokens,) * 6 + (P(),) * 4 + (P(("grp", "dp")),) * 2 + (tokens,) * 2 + (P("seq", "tp"), P())
    return jax.shard_map(
        local, mesh=mesh, in_specs=placed, out_specs=(tokens, tokens, P("grp")), check_vma=False
    )
```

time: 361 us -> 133 us (0.37)
  waiting for transfers between devices: 142 us -> 55.7 us
  blocking collectives: 53.5 us -> 0 us
  local copies, waits for them, and re-layouts: 57.3 us -> 4.36 us
  other arithmetic: 49.7 us -> 1.72 us
  Pallas kernels: 0 us -> 27 us
  matrix products: 25.7 us -> 0 us
  starting transfers between devices: 15.2 us -> 38 us
  between operations: 16.7 us -> 6.48 us
    all_gather x4 -> x0, waiting for transfers between devices: 124 us -> none  [the longest x1 118 us: local(): lax.all_gather(out_weight, 'seq', axis=0, tiled=True)]
    ppermute x0 -> x23, waiting for transfers between devices: none -> 55.7 us  [the longest x3 21.6 us: local(): lax.ppermute(text_rows[j], 'seq', shift(ring, -j))]
    unnamed x8 -> x0, other arithmetic: 40.4 us -> none
    ppermute x0 -> x23, starting transfers between devices: none -> 38 us  [the longest x4 10.1 us: all_sum(): lax.ppermute(value, axis, [(i, i ^ step) for i in range(size)])]
    psum x1 -> x0, blocking collectives: 31.3 us -> none  [local(): total_sum = lax.psum(partial_sum, ('seq', 'dp', 'tp'))]
    pallas_call x0 -> x5, Pallas kernels: none -> 27 us  [the longest x2 17.9 us: attend(): pl.pallas_call(functools.partial(attend_body, queries=len(blocks), pieces...]
    all_to_all x2 -> x0, blocking collectives: 22.2 us -> none  [the longest x1 17.8 us: local(): lax.all_to_all(head_output, 'seq', split_axis=1, concat_axis=2, tiled=True)]
    unnamed x42 -> x40, local copies, waits for them, and re-layouts: 22.5 us -> 4.36 us
  transfers between devices with their start and end apart: 7 -> 23, of which waited for: 4 -> 12; matrix products, arithmetic and copies ran while one was open for 16% -> 1% of each run, Pallas kernels for 0% -> 17%
where the time goes in v1:
time: 133 us
  waiting for transfers between devices  55.7 us (42%)
  starting transfers between devices  38 us (29%)
  Pallas kernels  27 us (20%)
  between operations  6.48 us (5%)
  local copies, waits for them, and re-layouts  4.36 us (3%)
  other arithmetic  1.72 us (1%)
    ppermute x3, waiting for transfers between devices, local(): lax.ppermute(text_rows[j], 'seq', shift(ring, -j))  21.6 us
    pallas_call x2, Pallas kernels, attend(): pl.pallas_call(functools.partial(attend_body, queries=len(blocks), pieces...  17.9 us
    ppermute x2, waiting for transfers between devices, exchange(): lax.ppermute(halfway, ('seq', 'tp'), both_ways(ring, cores, 1))  13.9 us
    ppermute x4, starting transfers between devices, all_sum(): lax.ppermute(value, axis, [(i, i ^ step) for i in range(size)])  10.1 us
    ppermute x3, starting transfers between devices, local(): lax.ppermute(text_rows[j], 'seq', shift(ring, -j))  8.32 us
    ppermute x3, starting transfers between devices, local(): carried = lax.ppermute(part, ('seq', 'tp'), both_ways(ring, cores, sign))  6.31 us
    ppermute x2, waiting for transfers between devices, exchange(): arrived[j] = lax.ppermute(blocks[j], 'seq', shift(ring, j))  6.29 us
    ppermute x2, waiting for transfers between devices, exchange(): lax.ppermute(halfway, ('seq', 'tp'), both_ways(ring, cores, middle - 1))  5.81 us
  transfers between devices with their start and end apart: 23, of which 12 were waited for; matrix products, arithmetic and copies ran while one was open for 1% of the time, Pallas kernels for 17%

profile of v1, /device:TPU:0, one launch (start us, length us, event | category | flops | bytes accessed | tf_op | source)
XLA Modules:
  0.0 133.1 jit_solution(14674209221627553468)
XLA Ops:
  0.6 0.6 collective-permute-start.10
  1.2 2.6 %pack_kv.1 = (bf16[2,144,512]{2,1,0:T(8,128)(2,1)}, bf16[2,144,512]{2,1,0:T(8,128)(2,1)}, bf16[2,144,512]{2,1,0:T(8,128)(2,1)}, bf16[2,144,512]{2,1,0:T(8,128)(2,1)}) custom-call(bf16[128,2048]{1,0:T(8,128)(2,1)} %bitcast.18, bf16[16,2048]{1,0:T(8,128)(2,1)} %bitcast.21, bf16[128,2048]{1,0:T(8,128)(2,1)} %bitcast.19, bf16[16,2048]{1,0:T(8,128)(2,1)} %bitcast.22, ...), custom_call_target="tpu_custom_call" | custom-call | tf_op jit(solution)/shard_map/pack_kv/pallas_call | solution.py:187
  3.8 2.6 %collective-permute-start.5 = (bf16[2,144,512]{2,1,0:T(8,128)(2,1)}, bf16[2,144,512]{2,1,0:T(8,128)(2,1)}, u32[]{:S(2)}, u32[]{:S(2)}) collective-permute-start(bf16[2,144,512]{2,1,0:T(8,128)(2,1)} %get-tuple-element.27), channel_id=1, source_target_pairs={{0,4},{1,13},{4,8},{5,1},{8,12},{9,5},{12,0},{13,9},{2,6},{3,15},{... | collective-permute-start | bytes 884744 | tf_op jit(solution)/shard_map/ppermute | solution.py:152
  6.4 2.1 %pack_q.1 = (bf16[144,512]{1,0:T(8,128)(2,1)}, bf16[144,512]{1,0:T(8,128)(2,1)}, bf16[144,512]{1,0:T(8,128)(2,1)}, bf16[144,512]{1,0:T(8,128)(2,1)}) custom-call(bf16[128,2048]{1,0:T(8,128)(2,1)} %bitcast.17, bf16[16,2048]{1,0:T(8,128)(2,1)} %bitcast.20, f32[1,128]{1,0:T(1,128)} %bitcast.25, f32[1,128]{1,0:T(1,128)} %bitcast.26), custom_call_target="tpu_custom_call" | custom-call | tf_op jit(solution)/shard_map/pack_q/pallas_call | solution.py:195
  8.5 1.6 %collective-permute-start.11 = (bf16[144,512]{1,0:T(8,128)(2,1)}, bf16[144,512]{1,0:T(8,128)(2,1)S(1)}, u32[]{:S(2)}, u32[]{:S(2)}) collective-permute-start(bf16[144,512]{1,0:T(8,128)(2,1)} %get-tuple-element.32), channel_id=1, source_target_pairs={{0,4},{1,13},{4,8},{5,1},{8,12},{9,5},{12,0},{13,9},{2,6},{3,15},{... | collective-permute-start | bytes 442376 | tf_op jit(solution)/shard_map/ppermute | solution.py:152
  10.1 1.6 %collective-permute-start.3 = (bf16[2,144,512]{2,1,0:T(8,128)(2,1)}, bf16[2,144,512]{2,1,0:T(8,128)(2,1)S(1)}, u32[]{:S(2)}, u32[]{:S(2)}) collective-permute-start(bf16[2,144,512]{2,1,0:T(8,128)(2,1)} %get-tuple-element.26), channel_id=1, source_target_pairs={{0,4},{4,8},{8,12},{12,0},{1,5},{5,9},{9,13},{13,1},{2,6},{6,10},{... | collective-permute-start | bytes 884744 | tf_op jit(solution)/shard_map/ppermute | solution.py:154
  11.7 2.3 %collective-permute-start.8 = (bf16[2,144,512]{2,1,0:T(8,128)(2,1)}, bf16[2,144,512]{2,1,0:T(8,128)(2,1)S(1)}, u32[]{:S(2)}, u32[]{:S(2)}) collective-permute-start(bf16[2,144,512]{2,1,0:T(8,128)(2,1)} %get-tuple-element.28), channel_id=1, source_target_pairs={{0,12},{4,0},{8,4},{12,8},{1,13},{5,1},{9,5},{13,9},{2,14},{6,2},{... | collective-permute-start | bytes 884744 | tf_op jit(solution)/shard_map/ppermute | solution.py:155
  13.9 2.7 %collective-permute-done.5 = bf16[2,144,512]{2,1,0:T(8,128)(2,1)} collective-permute-done((bf16[2,144,512]{2,1,0:T(8,128)(2,1)}, bf16[2,144,512]{2,1,0:T(8,128)(2,1)}, u32[]{:S(2)}, u32[]{:S(2)}) %collective-permute-start.5) | collective-permute-done | bytes 294944 | tf_op jit(solution)/shard_map/ppermute | solution.py:152
  16.6 0.0 collective-permute-start.6
  16.6 3.1 %collective-permute-done.11 = bf16[144,512]{1,0:T(8,128)(2,1)S(1)} collective-permute-done((bf16[144,512]{1,0:T(8,128)(2,1)}, bf16[144,512]{1,0:T(8,128)(2,1)S(1)}, u32[]{:S(2)}, u32[]{:S(2)}) %collective-permute-start.11) | collective-permute-done | bytes 147488 | tf_op jit(solution)/shard_map/ppermute | solution.py:152
  19.7 0.0 collective-permute-start.2
  19.8 6.3 %collective-permute-done.3.refs_5_.refs_3_ = bf16[2,144,512]{2,1,0:T(8,128)(2,1)S(1)} collective-permute-done((bf16[2,144,512]{2,1,0:T(8,128)(2,1)}, bf16[2,144,512]{2,1,0:T(8,128)(2,1)S(1)}, u32[]{:S(2)}, u32[]{:S(2)}) %collective-permute-start.3) | collective-permute-done | bytes 294944 | tf_op jit(solution)/shard_map/ppermute | solution.py:154
  26.0 0.0 collective-permute-start.4
  26.1 4.1 %collective-permute-done.8.refs_9_.refs_7_ = bf16[2,144,512]{2,1,0:T(8,128)(2,1)S(1)} collective-permute-done((bf16[2,144,512]{2,1,0:T(8,128)(2,1)}, bf16[2,144,512]{2,1,0:T(8,128)(2,1)S(1)}, u32[]{:S(2)}, u32[]{:S(2)}) %collective-permute-start.8) | collective-permute-done | bytes 294944 | tf_op jit(solution)/shard_map/ppermute | solution.py:155
  30.2 1.4 %collective-permute-start.9 = (bf16[2,144,512]{2,1,0:T(8,128)(2,1)S(1)}, bf16[2,144,512]{2,1,0:T(8,128)(2,1)S(1)}, u32[]{:S(2)}, u32[]{:S(2)}) collective-permute-start(bf16[2,144,512]{2,1,0:T(8,128)(2,1)S(1)} %collective-permute-done.8.refs_9_.refs_7_), channel_id=1, source_target_pairs={{1,0},{0,1},{3,2},{2,3},{5,4},{4,5},{7,6},{6,7},{9,8},{8,9},{11,10... | collective-permute-start | bytes 884744 | tf_op jit(solution)/shard_map/ppermute | solution.py:207
  31.6 7.0 %collective-permute-done.6.refs_7_.refs_5_ = bf16[2,144,512]{2,1,0:T(8,128)(2,1)S(1)} collective-permute-done((bf16[2,144,512]{2,1,0:T(8,128)(2,1)}, bf16[2,144,512]{2,1,0:T(8,128)(2,1)S(1)}, u32[]{:S(2)}, u32[]{:S(2)}) %collective-permute-start.6) | collective-permute-done | bytes 294944 | tf_op jit(solution)/shard_map/ppermute | solution.py:157
  38.6 0.0 collective-permute-start.7
  38.6 0.0 collective-permute-done.2.refs_4_.refs_2_
  38.6 0.1 collective-permute-start.12
  38.7 6.9 %collective-permute-done.12.refs_0_ = bf16[144,512]{1,0:T(8,128)(2,1)S(1)} collective-permute-done((bf16[144,512]{1,0:T(8,128)(2,1)S(1)}, bf16[144,512]{1,0:T(8,128)(2,1)S(1)}, u32[]{:S(2)}, u32[]{:S(2)}) %collective-permute-start.12) | collective-permute-done | bytes 147488 | tf_op jit(solution)/shard_map/ppermute | solution.py:157
  45.6 0.0 collective-permute-start
  45.6 0.0 collective-permute-done.4.refs_6_.refs_4_
  45.6 0.7 copy-done.13
  46.3 3.2 %collective-permute-start.1 = (bf16[144,512]{1,0:T(8,128)(2,1)}, bf16[144,512]{1,0:T(8,128)(2,1)}, u32[]{:S(2)}, u32[]{:S(2)}) collective-permute-start(bf16[144,512]{1,0:T(8,128)(2,1)} %get-tuple-element.24), channel_id=1, source_target_pairs={{0,12},{4,0},{8,4},{12,8},{1,13},{5,1},{9,5},{13,9},{2,14},{6,2},{... | collective-permute-start | bytes 442376 | tf_op jit(solution)/shard_map/ppermute | solution.py:155
  50.2 0.0 collective-permute-done.9.refs_10_.refs_8_
  50.2 0.0 collective-permute-done.7.refs_8_.refs_6_
  50.2 0.7 copy-done.9
  51.0 0.0 collective-permute-done.10.refs_12_.refs_10_
  51.0 0.0 copy-done.8
  51.0 1.2 copy-done
  52.2 6.3 %attend_far.1 = (bf16[128,3072]{1,0:T(8,128)(2,1)}, bf16[16,512]{1,0:T(8,128)(2,1)}) custom-call(s32[1]{0:T(128)S(6)} %copy.19.length, bf16[144,512]{1,0:T(8,128)(2,1)} %copy-done.13, bf16[2,144,512]{2,1,0:T(8,128)(2,1)} %get-tuple-element.25.refs_3_.refs_1_, bf16[2,144,512]{2,1,0:T(8,128)(2,1)} %copy-done.6, bf16[2,144,512]{2,1,0:T(8,128)(2,1)} %copy-done.3, ...), custom_call_target="tpu_custom_call" | custom-call | tf_op jit(solution)/shard_map/attend_far/pallas_call | solution.py:215
  58.5 0.0 collective-permute-start.13
  58.5 0.0 collective-permute-done.refs_1_
  58.5 0.0 collective-permute-done.1.refs_2_
  58.5 0.6 copy-done.12
  59.2 11.5 %attend_rest.1 = (f32[128,3072]{1,0:T(8,128)}, bf16[16,512]{1,0:T(8,128)(2,1)}, bf16[128,3072]{1,0:T(8,128)(2,1)}, bf16[16,512]{1,0:T(8,128)(2,1)}, bf16[128,3072]{1,0:T(8,128)(2,1)}, /*index=5*/bf16[16,512]{1,0:T(8,128)(2,1)}) custom-call(s32[1]{0:T(128)S(6)} %copy.19.length, bf16[144,512]{1,0:T(8,128)(2,1)} %get-tuple-element.22.refs_0_, ...), custom_call_target="tpu_custom_call" | custom-call | tf_op jit(solution)/shard_map/attend_rest/pallas_call | solution.py:215
  70.7 1.3 %broadcast_select_fusion = bf16[128,3072]{1,0:T(8,128)(2,1)S(1)} fusion(bf16[128,3072]{1,0:T(8,128)(2,1)} %get-tuple-element.30, bf16[128,3072]{1,0:T(8,128)(2,1)} %get-tuple-element.31, pred[]{:T(512)S(6)} %not.3), kind=kLoop, calls=%fused_computation.1 | loop fusion | flops 393216 | bytes 2359297 | tf_op jit(solution)/shard_map/jit(_where)/select_n | solution.py:277
  72.1 0.0 copy-start.18
  72.1 3.9 %collective-permute-start.15 = (bf16[128,3072]{1,0:T(8,128)(2,1)S(1)}, bf16[128,3072]{1,0:T(8,128)(2,1)S(1)}, u32[]{:S(2)}, u32[]{:S(2)}) collective-permute-start(bf16[128,3072]{1,0:T(8,128)(2,1)S(1)} %broadcast_select_fusion), channel_id=1, source_target_pairs={{0,12},{1,5},{4,0},{5,9},{8,4},{9,13},{12,8},{13,1},{2,14},{3,7},{... | collective-permute-start | bytes 2359304 | tf_op jit(solution)/shard_map/ppermute | solution.py:286
  76.0 0.8 collective-permute-done.13
  76.7 0.4 add_convert_fusion
  77.1 2.4 %collective-permute-start.14 = (bf16[128,3072]{1,0:T(8,128)(2,1)S(1)}, bf16[128,3072]{1,0:T(8,128)(2,1)S(1)}, u32[]{:S(2)}, u32[]{:S(2)}) collective-permute-start(bf16[128,3072]{1,0:T(8,128)(2,1)S(1)} %add_convert_fusion), channel_id=1, source_target_pairs={{0,4},{1,13},{4,8},{5,1},{8,12},{9,5},{12,0},{13,9},{2,6},{3,15},{... | collective-permute-start | bytes 2359304 | tf_op jit(solution)/shard_map/ppermute | solution.py:286
  79.6 3.1 %collective-permute-start.16 = (bf16[16,512]{1,0:T(8,128)(2,1)S(1)}, bf16[16,512]{1,0:T(8,128)(2,1)S(1)}, u32[]{:S(2)}, u32[]{:S(2)}) collective-permute-start(bf16[16,512]{1,0:T(8,128)(2,1)S(1)} %copy-done.19), channel_id=1, source_target_pairs={{0,4},{4,8},{8,12},{12,0},{1,5},{5,9},{9,13},{13,1},{2,6},{6,10},{... | collective-permute-start | bytes 49160 | tf_op jit(solution)/shard_map/ppermute | solution.py:290
  82.7 2.4 %collective-permute-start.17 = (bf16[16,512]{1,0:T(8,128)(2,1)S(1)}, bf16[16,512]{1,0:T(8,128)(2,1)S(1)}, u32[]{:S(2)}, u32[]{:S(2)}) collective-permute-start(bf16[16,512]{1,0:T(8,128)(2,1)S(1)} %copy-done.17), channel_id=1, source_target_pairs={{0,8},{4,12},{8,0},{12,4},{1,9},{5,13},{9,1},{13,5},{2,10},{6,14},... | collective-permute-start | bytes 49160 | tf_op jit(solution)/shard_map/ppermute | solution.py:290
  85.0 2.9 %collective-permute-start.18 = (bf16[16,512]{1,0:T(8,128)(2,1)S(1)}, bf16[16,512]{1,0:T(8,128)(2,1)S(1)}, u32[]{:S(2)}, u32[]{:S(2)}) collective-permute-start(bf16[16,512]{1,0:T(8,128)(2,1)S(1)} %copy-done.18), channel_id=1, source_target_pairs={{0,12},{4,0},{8,4},{12,8},{1,13},{5,1},{9,5},{13,9},{2,14},{6,2},{... | collective-permute-start | bytes 49160 | tf_op jit(solution)/shard_map/ppermute | solution.py:290
  88.5 21.5 %collective-permute-done.16.refs_6_ = bf16[16,512]{1,0:T(8,128)(2,1)S(1)} collective-permute-done((bf16[16,512]{1,0:T(8,128)(2,1)S(1)}, bf16[16,512]{1,0:T(8,128)(2,1)S(1)}, u32[]{:S(2)}, u32[]{:S(2)}) %collective-permute-start.16) | collective-permute-done | bytes 16416 | tf_op jit(solution)/shard_map/ppermute | solution.py:290
  110.1 0.0 collective-permute-done.17.refs_7_
  110.1 0.0 collective-permute-done.18.refs_8_
  110.1 0.0 collective-permute-done.15.refs_1_
  110.1 0.0 collective-permute-done.14.refs_0_
  110.2 0.5 copy-done.14
  110.7 0.0 copy-done.15
  110.7 0.0 copy-done.16
  110.7 0.3 copy-done.10
  111.0 0.3 copy-done.11
  111.3 4.3 %finish.1 = (bf16[128,3072]{1,0:T(8,128)(2,1)}, bf16[16,2048]{1,0:T(8,128)(2,1)}, f32[1,1]{1,0:T(1,128)}) custom-call(s32[1]{0:T(128)S(6)} %copy.20.strata, f32[128,3072]{1,0:T(8,128)} %get-tuple-element.29.own_part, bf16[128,3072]{1,0:T(8,128)(2,1)} %copy-done.11, bf16[128,3072]{1,0:T(8,128)(2,1)} %copy-done.10, bf16[128,3072]{1,0:T(8,128)(2,1)} %bitcast.15, ...), custom_call_target="tpu_custom_call" | custom-call | tf_op jit(solution)/shard_map/finish/pallas_call | solution.py:293
  115.6 0.6 collective-permute-start.19
  116.2 1.0 collective-permute-done.19
  118.4 2.8 %collective-permute-start.20 = (f32[1,1]{1,0:T(1,128)}, f32[1,1]{1,0:T(1,128)}, u32[]{:S(2)}, u32[]{:S(2)}) collective-permute-start(f32[1,1]{1,0:T(1,128)} %add.21), channel_id=1, source_target_pairs={{0,2},{2,0},{1,3},{3,1},{4,6},{6,4},{5,7},{7,5},{8,10},{10,8},{9,1... | collective-permute-start | bytes 20 | tf_op jit(solution)/shard_map/ppermute | solution.py:169
  121.3 0.7 collective-permute-done.20
  122.7 2.8 %collective-permute-start.21 = (f32[1,1]{1,0:T(1,128)}, f32[1,1]{1,0:T(1,128)}, u32[]{:S(2)}, u32[]{:S(2)}) collective-permute-start(f32[1,1]{1,0:T(1,128)} %add.22), channel_id=1, source_target_pairs={{0,4},{4,0},{8,12},{12,8},{1,5},{5,1},{9,13},{13,9},{2,6},{6,2},{1... | collective-permute-start | bytes 20 | tf_op jit(solution)/shard_map/ppermute | solution.py:169
  125.4 0.8 collective-permute-done.21
  126.9 3.8 %collective-permute-start.22 = (f32[1,1]{1,0:T(1,128)}, f32[1,1]{1,0:T(1,128)}, u32[]{:S(2)}, u32[]{:S(2)}) collective-permute-start(f32[1,1]{1,0:T(1,128)} %add.23), channel_id=1, source_target_pairs={{0,8},{4,12},{8,0},{12,4},{1,9},{5,13},{9,1},{13,5},{2,10},{6,14},... | collective-permute-start | bytes 20 | tf_op jit(solution)/shard_map/ppermute | solution.py:169
  130.7 0.7 collective-permute-done.22
  (29 shorter events, 0.1 us)
Async XLA Ops:
  0.6 50.3 %collective-permute-start.10 = (bf16[512,1536]{1,0:T(8,128)(2,1)}, bf16[512,1536]{1,0:T(8,128)(2,1)S(1)}, u32[]{:S(2)}, u32[]{:S(2)}) collective-permute-start(bf16[512,1536]{1,0:T(8,128)(2,1)} %refs_9_.1), channel_id=1, source_target_pairs={{1,0},{0,1},{3,2},{2,3},{5,4},{4,5},{7,6},{6,7},{9,8},{8,9},{11,10... | collective-permute-start | bytes 4718600 | tf_op jit(solution)/shard_map/ppermute | solution.py:249
  3.8 12.8 %collective-permute-start.5 = (bf16[2,144,512]{2,1,0:T(8,128)(2,1)}, bf16[2,144,512]{2,1,0:T(8,128)(2,1)}, u32[]{:S(2)}, u32[]{:S(2)}) collective-permute-start(bf16[2,144,512]{2,1,0:T(8,128)(2,1)} %get-tuple-element.27), channel_id=1, source_target_pairs={{0,4},{1,13},{4,8},{5,1},{8,12},{9,5},{12,0},{13,9},{2,6},{3,15},{... | collective-permute-start | bytes 884744 | tf_op jit(solution)/shard_map/ppermute | solution.py:152
  8.5 11.2 %collective-permute-start.11 = (bf16[144,512]{1,0:T(8,128)(2,1)}, bf16[144,512]{1,0:T(8,128)(2,1)S(1)}, u32[]{:S(2)}, u32[]{:S(2)}) collective-permute-start(bf16[144,512]{1,0:T(8,128)(2,1)} %get-tuple-element.32), channel_id=1, source_target_pairs={{0,4},{1,13},{4,8},{5,1},{8,12},{9,5},{12,0},{13,9},{2,6},{3,15},{... | collective-permute-start | bytes 442376 | tf_op jit(solution)/shard_map/ppermute | solution.py:152
  10.1 15.9 %collective-permute-start.3 = (bf16[2,144,512]{2,1,0:T(8,128)(2,1)}, bf16[2,144,512]{2,1,0:T(8,128)(2,1)S(1)}, u32[]{:S(2)}, u32[]{:S(2)}) collective-permute-start(bf16[2,144,512]{2,1,0:T(8,128)(2,1)} %get-tuple-element.26), channel_id=1, source_target_pairs={{0,4},{4,8},{8,12},{12,0},{1,5},{5,9},{9,13},{13,1},{2,6},{6,10},{... | collective-permute-start | bytes 884744 | tf_op jit(solution)/shard_map/ppermute | solution.py:154
  11.7 18.5 %collective-permute-start.8 = (bf16[2,144,512]{2,1,0:T(8,128)(2,1)}, bf16[2,144,512]{2,1,0:T(8,128)(2,1)S(1)}, u32[]{:S(2)}, u32[]{:S(2)}) collective-permute-start(bf16[2,144,512]{2,1,0:T(8,128)(2,1)} %get-tuple-element.28), channel_id=1, source_target_pairs={{0,12},{4,0},{8,4},{12,8},{1,13},{5,1},{9,5},{13,9},{2,14},{6,2},{... | collective-permute-start | bytes 884744 | tf_op jit(solution)/shard_map/ppermute | solution.py:155
  16.6 22.0 %collective-permute-start.6 = (bf16[2,144,512]{2,1,0:T(8,128)(2,1)}, bf16[2,144,512]{2,1,0:T(8,128)(2,1)S(1)}, u32[]{:S(2)}, u32[]{:S(2)}) collective-permute-start(bf16[2,144,512]{2,1,0:T(8,128)(2,1)} %collective-permute-done.5), channel_id=1, source_target_pairs={{0,4},{1,13},{4,8},{5,1},{8,12},{9,5},{12,0},{13,9},{2,6},{3,15},{... | collective-permute-start | bytes 884744 | tf_op jit(solution)/shard_map/ppermute | solution.py:157
  19.7 18.9 %collective-permute-start.2 = (bf16[2,144,512]{2,1,0:T(8,128)(2,1)}, bf16[2,144,512]{2,1,0:T(8,128)(2,1)S(1)}, u32[]{:S(2)}, u32[]{:S(2)}) collective-permute-start(bf16[2,144,512]{2,1,0:T(8,128)(2,1)} %get-tuple-element.25.refs_3_.refs_1_), channel_id=1, source_target_pairs={{1,0},{0,1},{3,2},{2,3},{5,4},{4,5},{7,6},{6,7},{9,8},{8,9},{11,10... | collective-permute-start | bytes 884744 | tf_op jit(solution)/shard_map/ppermute | solution.py:207
  26.0 24.9 %copy-start.3 = (bf16[2,144,512]{2,1,0:T(8,128)(2,1)}, bf16[2,144,512]{2,1,0:T(8,128)(2,1)S(1)}, u32[]{:S(2)}) copy-start(bf16[2,144,512]{2,1,0:T(8,128)(2,1)S(1)} %collective-permute-done.3.refs_5_.refs_3_) | copy-start | bytes 884740
  26.0 19.6 %collective-permute-start.4 = (bf16[2,144,512]{2,1,0:T(8,128)(2,1)S(1)}, bf16[2,144,512]{2,1,0:T(8,128)(2,1)S(1)}, u32[]{:S(2)}, u32[]{:S(2)}) collective-permute-start(bf16[2,144,512]{2,1,0:T(8,128)(2,1)S(1)} %collective-permute-done.3.refs_5_.refs_3_), channel_id=1, source_target_pairs={{1,0},{0,1},{3,2},{2,3},{5,4},{4,5},{7,6},{6,7},{9,8},{8,9},{11,10... | collective-permute-start | bytes 884744 | tf_op jit(solution)/shard_map/ppermute | solution.py:207
  30.2 20.8 %copy-start.4 = (bf16[2,144,512]{2,1,0:T(8,128)(2,1)}, bf16[2,144,512]{2,1,0:T(8,128)(2,1)S(1)}, u32[]{:S(2)}) copy-start(bf16[2,144,512]{2,1,0:T(8,128)(2,1)S(1)} %collective-permute-done.8.refs_9_.refs_7_) | copy-start | bytes 884740
  30.2 20.0 %collective-permute-start.9 = (bf16[2,144,512]{2,1,0:T(8,128)(2,1)S(1)}, bf16[2,144,512]{2,1,0:T(8,128)(2,1)S(1)}, u32[]{:S(2)}, u32[]{:S(2)}) collective-permute-start(bf16[2,144,512]{2,1,0:T(8,128)(2,1)S(1)} %collective-permute-done.8.refs_9_.refs_7_), channel_id=1, source_target_pairs={{1,0},{0,1},{3,2},{2,3},{5,4},{4,5},{7,6},{6,7},{9,8},{8,9},{11,10... | collective-permute-start | bytes 884744 | tf_op jit(solution)/shard_map/ppermute | solution.py:207
  38.6 12.3 %copy-start.5 = (bf16[2,144,512]{2,1,0:T(8,128)(2,1)}, bf16[2,144,512]{2,1,0:T(8,128)(2,1)S(1)}, u32[]{:S(2)}) copy-start(bf16[2,144,512]{2,1,0:T(8,128)(2,1)S(1)} %collective-permute-done.6.refs_7_.refs_5_) | copy-start | bytes 884740
  38.6 11.6 %collective-permute-start.7 = (bf16[2,144,512]{2,1,0:T(8,128)(2,1)S(1)}, bf16[2,144,512]{2,1,0:T(8,128)(2,1)S(1)}, u32[]{:S(2)}, u32[]{:S(2)}) collective-permute-start(bf16[2,144,512]{2,1,0:T(8,128)(2,1)S(1)} %collective-permute-done.6.refs_7_.refs_5_), channel_id=1, source_target_pairs={{1,0},{0,1},{3,2},{2,3},{5,4},{4,5},{7,6},{6,7},{9,8},{8,9},{11,10... | collective-permute-start | bytes 884744 | tf_op jit(solution)/shard_map/ppermute | solution.py:207
  38.6 12.3 %copy-start.6 = (bf16[2,144,512]{2,1,0:T(8,128)(2,1)}, bf16[2,144,512]{2,1,0:T(8,128)(2,1)S(1)}, u32[]{:S(2)}) copy-start(bf16[2,144,512]{2,1,0:T(8,128)(2,1)S(1)} %collective-permute-done.2.refs_4_.refs_2_) | copy-start | bytes 884740
  38.6 7.0 %collective-permute-start.12 = (bf16[144,512]{1,0:T(8,128)(2,1)S(1)}, bf16[144,512]{1,0:T(8,128)(2,1)S(1)}, u32[]{:S(2)}, u32[]{:S(2)}) collective-permute-start(bf16[144,512]{1,0:T(8,128)(2,1)S(1)} %collective-permute-done.11), channel_id=1, source_target_pairs={{0,4},{1,13},{4,8},{5,1},{8,12},{9,5},{12,0},{13,9},{2,6},{3,15},{... | collective-permute-start | bytes 442376 | tf_op jit(solution)/shard_map/ppermute | solution.py:157
  45.6 0.7 copy-start.13
  45.6 12.9 %collective-permute-start = (bf16[144,512]{1,0:T(8,128)(2,1)}, bf16[144,512]{1,0:T(8,128)(2,1)S(1)}, u32[]{:S(2)}, u32[]{:S(2)}) collective-permute-start(bf16[144,512]{1,0:T(8,128)(2,1)} %get-tuple-element.23), channel_id=1, source_target_pairs={{0,4},{4,8},{8,12},{12,0},{1,5},{5,9},{9,13},{13,1},{2,6},{6,10},{... | collective-permute-start | bytes 442376 | tf_op jit(solution)/shard_map/ppermute | solution.py:154
  46.3 4.7 %copy-start.7 = (bf16[2,144,512]{2,1,0:T(8,128)(2,1)}, bf16[2,144,512]{2,1,0:T(8,128)(2,1)S(1)}, u32[]{:S(2)}) copy-start(bf16[2,144,512]{2,1,0:T(8,128)(2,1)S(1)} %collective-permute-done.4.refs_6_.refs_4_) | copy-start | bytes 884740
  46.3 12.2 %collective-permute-start.1 = (bf16[144,512]{1,0:T(8,128)(2,1)}, bf16[144,512]{1,0:T(8,128)(2,1)}, u32[]{:S(2)}, u32[]{:S(2)}) collective-permute-start(bf16[144,512]{1,0:T(8,128)(2,1)} %get-tuple-element.24), channel_id=1, source_target_pairs={{0,12},{4,0},{8,4},{12,8},{1,13},{5,1},{9,5},{13,9},{2,14},{6,2},{... | collective-permute-start | bytes 442376 | tf_op jit(solution)/shard_map/ppermute | solution.py:155
  50.2 0.8 copy-start.8
  50.2 0.7 copy-start.9
  51.0 1.2 copy-start
  58.5 18.3 %collective-permute-start.13 = (bf16[128,3072]{1,0:T(8,128)(2,1)}, bf16[128,3072]{1,0:T(8,128)(2,1)S(1)}, u32[]{:S(2)}, u32[]{:S(2)}) collective-permute-start(bf16[128,3072]{1,0:T(8,128)(2,1)} %get-tuple-element.33), channel_id=1, source_target_pairs={{0,4},{1,13},{4,8},{5,1},{8,12},{9,5},{12,0},{13,9},{2,6},{3,15},{... | collective-permute-start | bytes 2359304 | tf_op jit(solution)/shard_map/ppermute | solution.py:286
  58.5 0.7 copy-start.12
  70.7 6.1 %copy-start.1 = (bf16[128,3072]{1,0:T(8,128)(2,1)S(1)}, bf16[128,3072]{1,0:T(8,128)(2,1)}, u32[]{:S(2)}) copy-start(bf16[128,3072]{1,0:T(8,128)(2,1)} %get-tuple-element.31) | copy-start | bytes 2359300
  70.7 6.1 %copy-start.2 = (bf16[128,3072]{1,0:T(8,128)(2,1)S(1)}, bf16[128,3072]{1,0:T(8,128)(2,1)}, u32[]{:S(2)}) copy-start(bf16[128,3072]{1,0:T(8,128)(2,1)} %get-tuple-element.30) | copy-start | bytes 2359300
  72.1 7.5 %copy-start.19 = (bf16[16,512]{1,0:T(8,128)(2,1)S(1)}, bf16[16,512]{1,0:T(8,128)(2,1)}, u32[]{:S(2)}) copy-start(bf16[16,512]{1,0:T(8,128)(2,1)} %get-tuple-element.35) | copy-start | bytes 49156
  72.1 10.6 %copy-start.17 = (bf16[16,512]{1,0:T(8,128)(2,1)S(1)}, bf16[16,512]{1,0:T(8,128)(2,1)}, u32[]{:S(2)}) copy-start(bf16[16,512]{1,0:T(8,128)(2,1)} %get-tuple-element.36) | copy-start | bytes 49156
  72.1 13.0 %copy-start.18 = (bf16[16,512]{1,0:T(8,128)(2,1)S(1)}, bf16[16,512]{1,0:T(8,128)(2,1)}, u32[]{:S(2)}) copy-start(bf16[16,512]{1,0:T(8,128)(2,1)} %get-tuple-element.37) | copy-start | bytes 49156
  72.1 38.0 %collective-permute-start.15 = (bf16[128,3072]{1,0:T(8,128)(2,1)S(1)}, bf16[128,3072]{1,0:T(8,128)(2,1)S(1)}, u32[]{:S(2)}, u32[]{:S(2)}) collective-permute-start(bf16[128,3072]{1,0:T(8,128)(2,1)S(1)} %broadcast_select_fusion), channel_id=1, source_target_pairs={{0,12},{1,5},{4,0},{5,9},{8,4},{9,13},{12,8},{13,1},{2,14},{3,7},{... | collective-permute-start | bytes 2359304 | tf_op jit(solution)/shard_map/ppermute | solution.py:286
  77.1 33.0 %collective-permute-start.14 = (bf16[128,3072]{1,0:T(8,128)(2,1)S(1)}, bf16[128,3072]{1,0:T(8,128)(2,1)S(1)}, u32[]{:S(2)}, u32[]{:S(2)}) collective-permute-start(bf16[128,3072]{1,0:T(8,128)(2,1)S(1)} %add_convert_fusion), channel_id=1, source_target_pairs={{0,4},{1,13},{4,8},{5,1},{8,12},{9,5},{12,0},{13,9},{2,6},{3,15},{... | collective-permute-start | bytes 2359304 | tf_op jit(solution)/shard_map/ppermute | solution.py:286
  79.6 30.5 %collective-permute-start.16 = (bf16[16,512]{1,0:T(8,128)(2,1)S(1)}, bf16[16,512]{1,0:T(8,128)(2,1)S(1)}, u32[]{:S(2)}, u32[]{:S(2)}) collective-permute-start(bf16[16,512]{1,0:T(8,128)(2,1)S(1)} %copy-done.19), channel_id=1, source_target_pairs={{0,4},{4,8},{8,12},{12,0},{1,5},{5,9},{9,13},{13,1},{2,6},{6,10},{... | collective-permute-start | bytes 49160 | tf_op jit(solution)/shard_map/ppermute | solution.py:290
  82.7 27.4 %collective-permute-start.17 = (bf16[16,512]{1,0:T(8,128)(2,1)S(1)}, bf16[16,512]{1,0:T(8,128)(2,1)S(1)}, u32[]{:S(2)}, u32[]{:S(2)}) collective-permute-start(bf16[16,512]{1,0:T(8,128)(2,1)S(1)} %copy-done.17), channel_id=1, source_target_pairs={{0,8},{4,12},{8,0},{12,4},{1,9},{5,13},{9,1},{13,5},{2,10},{6,14},... | collective-permute-start | bytes 49160 | tf_op jit(solution)/shard_map/ppermute | solution.py:290
  85.0 25.1 %collective-permute-start.18 = (bf16[16,512]{1,0:T(8,128)(2,1)S(1)}, bf16[16,512]{1,0:T(8,128)(2,1)S(1)}, u32[]{:S(2)}, u32[]{:S(2)}) collective-permute-start(bf16[16,512]{1,0:T(8,128)(2,1)S(1)} %copy-done.18), channel_id=1, source_target_pairs={{0,12},{4,0},{8,4},{12,8},{1,13},{5,1},{9,5},{13,9},{2,14},{6,2},{... | collective-permute-start | bytes 49160 | tf_op jit(solution)/shard_map/ppermute | solution.py:290
  110.1 0.6 copy-start.14
  110.1 0.6 copy-start.15
  110.1 0.6 copy-start.16
  110.1 0.9 copy-start.10
  110.1 1.1 copy-start.11
  115.6 1.6 %collective-permute-start.19 = (f32[1,1]{1,0:T(1,128)}, f32[1,1]{1,0:T(1,128)}, u32[]{:S(2)}, u32[]{:S(2)}) collective-permute-start(f32[1,1]{1,0:T(1,128)} %get-tuple-element.40), channel_id=1, source_target_pairs={{0,1},{1,0},{2,3},{3,2},{4,5},{5,4},{6,7},{7,6},{8,9},{9,8},{10,11... | collective-permute-start | bytes 20 | tf_op jit(solution)/shard_map/ppermute | solution.py:169
  118.4 3.6 %collective-permute-start.20 = (f32[1,1]{1,0:T(1,128)}, f32[1,1]{1,0:T(1,128)}, u32[]{:S(2)}, u32[]{:S(2)}) collective-permute-start(f32[1,1]{1,0:T(1,128)} %add.21), channel_id=1, source_target_pairs={{0,2},{2,0},{1,3},{3,1},{4,6},{6,4},{5,7},{7,5},{8,10},{10,8},{9,1... | collective-permute-start | bytes 20 | tf_op jit(solution)/shard_map/ppermute | solution.py:169
  122.7 3.6 %collective-permute-start.21 = (f32[1,1]{1,0:T(1,128)}, f32[1,1]{1,0:T(1,128)}, u32[]{:S(2)}, u32[]{:S(2)}) collective-permute-start(f32[1,1]{1,0:T(1,128)} %add.22), channel_id=1, source_target_pairs={{0,4},{4,0},{8,12},{12,8},{1,5},{5,1},{9,13},{13,9},{2,6},{6,2},{1... | collective-permute-start | bytes 20 | tf_op jit(solution)/shard_map/ppermute | solution.py:169
  126.9 4.5 %collective-permute-start.22 = (f32[1,1]{1,0:T(1,128)}, f32[1,1]{1,0:T(1,128)}, u32[]{:S(2)}, u32[]{:S(2)}) collective-permute-start(f32[1,1]{1,0:T(1,128)} %add.23), channel_id=1, source_target_pairs={{0,8},{4,12},{8,0},{12,4},{1,9},{5,13},{9,1},{13,5},{2,10},{6,14},... | collective-permute-start | bytes 20 | tf_op jit(solution)/shard_map/ppermute | solution.py:169
